TPU v7x, 32 devices: a whole 2x2x4 slice. The times are simulated.
32 devices in a mesh: row: 8 (over z, x), col: 4 (over y, core).
Axes of the slice: x: 2, y: 2, z: 4, core: 2. Of those that a mesh axis runs over, the one named last changes fastest.
Arguments:
- gradients: bfloat16 [32, 2, 524288], P(('row', 'col')), may hold values from -96 to 96
- master_params: float32 [2, 524288], P(None, ('row', 'col')), may hold values from -0.1 to 0.1
- first_moment: float32 [2, 524288], P(None, ('row', 'col')), may hold values from -3 to 3
- second_moment: float32 [2, 524288], P(None, ('row', 'col')), may hold values from 0.05 to 5
Outputs:
- new_master: float32 [2, 524288], P(None, ('row', 'col'))
- new_first: float32 [2, 524288], P(None, ('row', 'col'))
- new_second: float32 [2, 524288], P(None, ('row', 'col'))
- new_weights: bfloat16 [2, 524288], replicated
All inputs are finite; a program needn't handle non-finite values.
Results may differ from a plain program's by a relative error of at most 0.009.
Values may be sent and summed in bfloat16 or wider, within the bound.
A program may use at most 64 MiB of HBM per device.

v0:
```python
import jax
import jax.numpy as jnp
from jax import lax
from jax.sharding import PartitionSpec as P

beta_one = 0.9
beta_two = 0.95
learn_rate = 0.001
decay_rate = 0.1
epsilon = 1e-08
adam_step = 10.0


def adam_update(mean_grad, master_params, first_moment, second_moment):
    new_first = beta_one * first_moment + (1.0 - beta_one) * mean_grad
    new_second = beta_two * second_moment + (1.0 - beta_two) * mean_grad * mean_grad
    first_hat = new_first / (1.0 - beta_one**adam_step)
    second_hat = new_second / (1.0 - beta_two**adam_step)
    new_master = master_params - learn_rate * (
        first_hat / (jnp.sqrt(second_hat) + epsilon) + decay_rate * master_params
    )
    return (new_master, new_first, new_second)


def shards(gradients, master_params, first_moment, second_moment):
    row_count = lax.axis_size("row")
    col_count = lax.axis_size("col")
    layers = gradients.shape[1]
    slice_len = gradients.shape[2]
    portion = slice_len // (row_count * col_count)
    summed_grad = gradients[0].astype(jnp.float32)
    blocks = summed_grad.reshape(layers, row_count * col_count, portion)
    reduced = lax.psum_scatter(blocks, ("row", "col"), scatter_dimension=1, tiled=True).reshape(
        layers, portion
    )
    mean_grad = reduced / (row_count * col_count)
    new_master, new_first, new_second = adam_update(
        mean_grad, master_params, first_moment, second_moment
    )
    rounded = new_master.astype(jnp.bfloat16)
    pieces = rounded.reshape(layers, 1, portion)
    new_weights = lax.all_gather(pieces, ("row", "col"), axis=1, tiled=True).reshape(
        layers, slice_len
    )
    return (new_master, new_first, new_second, new_weights)


def solution(mesh):
    in_specs = (
        P(("row", "col"), None, None),
        P(None, ("row", "col")),
        P(None, ("row", "col")),
        P(None, ("row", "col")),
    )
    out_specs = (P(None, ("row", "col")), P(None, ("row", "col")), P(None, ("row", "col")), P())
    return jax.shard_map(shards, mesh=mesh, in_specs=in_specs, out_specs=out_specs, check_vma=False)
```

profile of v0, /device:TPU:0, one launch (start us, length us, event | category | flops | bytes accessed | tf_op | source)
XLA Modules:
  0.0 170.3 jit_solution(15936403271155422)
XLA Ops:
  7.2 0.0 all-gather.3.cloned.1.call-start
  7.2 0.0 copy-start
  7.2 0.0 copy-start.1
  7.2 0.0 copy-start.2
  7.2 94.1 %all-reduce.2 = f32[2,32,16384]{2,0,1:T(2,128)} all-reduce(bf16[2,32,16384]{2,0,1:T(2,128)(2,1)} %bitcast.8), channel_id=3, replica_groups=mesh['row'=8,'col'=4] {'row','col'}, use_global_device_ids=true, to_apply=%region_0.0.clone | all-reduce | flops 1048576 | bytes 6291456
  101.3 0.0 copy-done
  101.3 0.0 copy-done.1
  101.3 0.0 copy-done.2
  101.3 2.1 %fusion = (bf16[2,16384]{1,0:T(2,128)(2,1)}, f32[2,16384]{1,0:T(2,128)}, f32[2,16384]{1,0:T(2,128)}, f32[2,16384]{1,0:T(2,128)}) fusion(f32[2,16384]{1,0:T(2,128)S(1)} %copy-done, f32[2,32,16384]{2,0,1:T(2,128)} %all-reduce.2, u32[]{:T(128)S(6)} %add.23, f32[2,16384]{1,0:T(2,128)S(1)} %copy-done.1, f32[2,16384]{1,0:T(2,128)S(1)} %copy-done.2), kind=kLoop, calls=%fused_computation.3 | loop fusion | flops 557056 | bytes 983044 | tf_op jit(solution)/shard_map/convert_element_type | solution.py:40
  103.4 0.0 all-gather.3.cloned.1.call-update
  103.5 55.6 %all-gather.3.cloned.1.call-done = bf16[2,524288]{1,0:T(2,128)(2,1)} async-done(((bf16[2,16384]{1,0:T(2,128)(2,1)}), bf16[2,524288]{1,0:T(2,128)(2,1)}) %all-gather.3.cloned.1.call-update) | async-done | bytes 2097168 | tf_op jit(solution)/shard_map/all_gather | solution.py:42
  159.1 4.4 %copy.12 = bf16[2,524288]{1,0:T(2,128)(2,1)} copy(bf16[2,524288]{1,0:T(2,128)(2,1)} %all-gather.3.cloned.1.call-done) | data formatting | bytes 4194304
Async XLA Ops:
  7.2 151.9 %all-gather.3.cloned.1.call-start = ((), (), s32[]{:S(2)}) async-start(), calls=%async_computation | async-start | bytes 2162688 | tf_op jit(solution)/shard_map/all_gather | solution.py:42
  7.2 94.1 %copy-start = (f32[2,16384]{1,0:T(2,128)S(1)}, f32[2,16384]{1,0:T(2,128)}, u32[]{:S(2)}) copy-start(f32[2,16384]{1,0:T(2,128)} %param.5) | copy-start | bytes 393220
  7.2 94.1 %copy-start.1 = (f32[2,16384]{1,0:T(2,128)S(1)}, f32[2,16384]{1,0:T(2,128)}, u32[]{:S(2)}) copy-start(f32[2,16384]{1,0:T(2,128)} %param.6) | copy-start | bytes 393220
  7.2 94.1 %copy-start.2 = (f32[2,16384]{1,0:T(2,128)S(1)}, f32[2,16384]{1,0:T(2,128)}, u32[]{:S(2)}) copy-start(f32[2,16384]{1,0:T(2,128)} %param.7) | copy-start | bytes 393220
Sparse Core Ops, SparseCore 0:
  103.6 55.4 all-gather.2
where the time goes:
time: 171 us; the launch traced here: 170 us
  blocking collectives  94.1 us (55%)
  waiting for transfers between devices  55.6 us (33%)
  between operations  14.1 us (8%)
  local copies, waits for them, and re-layouts  4.44 us (3%)
  other arithmetic  2.1 us (1%)
    unnamed x1, blocking collectives  94.1 us
    all_gather x1, waiting for transfers between devices, shards(): lax.all_gather(pieces, ('row', 'col'), axis=1, tiled=True)  55.6 us
    unnamed x7, local copies, waits for them, and re-layouts  4.44 us
  transfers between devices with their start and end apart: 1, of which 1 were waited for; matrix products, arithmetic and copies ran while one was open for 0% of the time, Pallas kernels for 0%

commit v1 on v0

v1 whole, which is shorter than its diff:
```python
import functools

import jax
import jax.numpy as jnp
import numpy as np
from jax import lax
from jax.experimental import pallas as pl
from jax.experimental.pallas import tpu as pltpu
from jax.sharding import PartitionSpec as P

beta_one = 0.9
beta_two = 0.95
learn_rate = 0.001
decay_rate = 0.1
epsilon = 1e-08
adam_step = 10.0

LANES = 128
FLOWS = 4
MESH = pl.DeviceIdType.MESH


def adam_update(mean_grad, master_params, first_moment, second_moment):
    new_first = beta_one * first_moment + (1.0 - beta_one) * mean_grad
    new_second = beta_two * second_moment + (1.0 - beta_two) * mean_grad * mean_grad
    first_hat = new_first / (1.0 - beta_one**adam_step)
    second_hat = new_second / (1.0 - beta_two**adam_step)
    new_master = master_params - learn_rate * (
        first_hat / (jnp.sqrt(second_hat) + epsilon) + decay_rate * master_params
    )
    return (new_master, new_first, new_second)


def factors(n):
    out = []
    while n > 1:
        k = next(k for k in (4, 2, *range(3, n + 1)) if n % k == 0)
        out.append(k)
        n //= k
    return out


def digits_of(rows, cols):
    core = [2] if cols % 2 == 0 else []
    found = []
    for axis, sizes in (("row", factors(rows)), ("col", factors(cols // (2 if core else 1)) + core)):
        stride = int(np.prod(sizes, dtype=np.int64))
        for size in sizes:
            stride //= size
            found.append((axis, size, stride))
    return found


def orders_of(digits):
    last = len(digits) - 1
    row_at = [i for i in range(last) if digits[i][0] == "row"]
    col_at = [i for i in range(last) if digits[i][0] == "col"]
    x, y = row_at[-1:], col_at[:1]
    rest = col_at[1:] + row_at[:-1]
    return ([last] + x + y + rest, [last] + y + x + rest)


def kernel(digits, flow_orders, r, grad, master, first, second, new_master, new_first, new_second, weights, scratch):
    count = len(digits)
    devices = int(np.prod([d[1] for d in digits]))
    at = {axis: lax.axis_index(axis) for axis in ("row", "col")}
    mine = [lax.rem(at[axis] // stride, size) for axis, size, stride in digits]

    def peer(digit, t):
        axis, size, stride = digits[digit]
        value = lax.rem(mine[digit] + t, size)
        ids = dict(at)
        ids[axis] = at[axis] + (value - mine[digit]) * stride
        return value, (ids["row"], ids["col"])

    flows = len(flow_orders)
    rows = [pl.ds(f * r, r) for f in range(flows)]

    loads = []
    for f in range(flows):
        digit = flow_orders[f][0]
        where = tuple(mine[i] if i == digit else slice(None) for i in range(count)) + (rows[f],)
        copy = pltpu.make_async_copy(grad.at[where], scratch["own"].at[f], scratch["load_sem"].at[f])
        copy.start()
        loads.append(copy)
    states = []
    for i, (src, name) in enumerate(((master, "master"), (first, "first"), (second, "second"))):
        copy = pltpu.make_async_copy(src, scratch[name], scratch["load_sem"].at[flows + i])
        copy.start()
        states.append(copy)

    barrier = pltpu.get_barrier_semaphore()
    greeted = 0
    for digit in range(count):
        for t in range(1, digits[digit][1]):
            pl.semaphore_signal(barrier, inc=1, device_id=peer(digit, t)[1], device_id_type=MESH)
            greeted += 1
    pl.semaphore_wait(barrier, greeted)

    sent = []
    pending = {}

    def send(f, step, digit, t, src, dst, device):
        copy = pltpu.make_async_remote_copy(
            src_ref=src,
            dst_ref=dst,
            send_sem=scratch["send_sem"].at[f, step, t - 1],
            recv_sem=scratch["recv_sem"].at[f, step, t - 1],
            device_id=device,
            device_id_type=MESH,
        )
        copy.start()
        sent.append(copy)
        pending.setdefault((f, step), []).append(copy)

    def scatter(f, p):
        digit = flow_orders[f][p]
        left = sorted(flow_orders[f][p:])
        for t in range(1, digits[digit][1]):
            value, device = peer(digit, t)
            where = tuple(value if i == digit else slice(None) for i in left)
            src = grad.at[where + (rows[f],)] if p == 0 else scratch[f"sum{f}_{p}"].at[where]
            send(f, p, digit, t, src, scratch[f"got{f}_{p}"].at[t - 1], device)

    def gather(f, p):
        digit = flow_orders[f][p]
        have = set(flow_orders[f][p + 1 :])
        where = tuple(slice(None) if i in have else mine[i] for i in range(count)) + (rows[f],)
        for t in range(1, digits[digit][1]):
            send(f, 2 * count - 1 - p, digit, t, weights.at[where], weights.at[where], peer(digit, t)[1])

    def arrived(f, step):
        for copy in pending[(f, step)]:
            copy.wait_recv()

    for f in range(flows):
        scatter(f, 0)
    for p in range(count):
        for f in range(flows):
            digit = flow_orders[f][p]
            left = sorted(flow_orders[f][p:])
            after = sorted(flow_orders[f][p + 1 :])
            if p == 0:
                loads[f].wait()
            arrived(f, p)
            got = scratch[f"got{f}_{p}"]
            last = p == count - 1
            for idx in np.ndindex(*(digits[i][1] for i in after)):
                if p == 0:
                    total = scratch["own"][(f,) + idx].astype(jnp.float32)
                else:
                    place = dict(zip(after, idx))
                    total = scratch[f"sum{f}_{p}"][
                        tuple(mine[digit] if i == digit else place[i] for i in left)
                    ].astype(jnp.float32)
                for t in range(digits[digit][1] - 1):
                    total += got[(t,) + idx].astype(jnp.float32)
                if not last:
                    scratch[f"sum{f}_{p + 1}"][idx] = total.astype(jnp.bfloat16)
            if not last:
                scatter(f, p + 1)
                continue
            if f == 0:
                for copy in states:
                    copy.wait()
            updated, moment, variance = adam_update(
                total / devices, scratch["master"][rows[f], :], scratch["first"][rows[f], :], scratch["second"][rows[f], :]
            )
            weights[tuple(mine) + (rows[f],)] = updated.astype(jnp.bfloat16)
            gather(f, count - 1)
            new_master[rows[f], :] = updated
            new_first[rows[f], :] = moment
            new_second[rows[f], :] = variance
    for p in reversed(range(count)):
        for f in range(flows):
            arrived(f, 2 * count - 1 - p)
            if p > 0:
                gather(f, p - 1)
    for copy in sent:
        copy.wait_send()


def to_rows(x):
    layers, length = x.shape
    return x.reshape(layers, length // LANES, LANES).transpose(1, 0, 2).reshape(layers * length // LANES, LANES)


def from_rows(x, layers):
    total = x.shape[0]
    return x.reshape(total // layers, layers, LANES).transpose(1, 0, 2).reshape(layers, total // layers * LANES)


def shards(digits, gradients, master_params, first_moment, second_moment):
    count = len(digits)
    sizes = tuple(d[1] for d in digits)
    devices = int(np.prod(sizes))
    layers = gradients.shape[1]
    grad = to_rows(gradients[0])
    block = grad.shape[0] // devices
    flows = next(n for n in (FLOWS, 2, 1) if block % n == 0 and (block // n) % 16 == 0)
    r = block // flows
    orders = orders_of(digits)
    flow_orders = [orders[f % len(orders)] for f in range(flows)]

    most = max(sizes) - 1
    scratch = {
        "own": pltpu.VMEM((flows,) + sizes[:-1] + (r, LANES), jnp.bfloat16),
        "load_sem": pltpu.SemaphoreType.DMA((flows + 3,)),
        "send_sem": pltpu.SemaphoreType.DMA((flows, 2 * count, most)),
        "recv_sem": pltpu.SemaphoreType.DMA((flows, 2 * count, most)),
    }
    for name in ("master", "first", "second"):
        scratch[name] = pltpu.VMEM((block, LANES), jnp.float32)
    for f, order in enumerate(flow_orders):
        for p in range(count):
            left = tuple(sizes[i] for i in sorted(order[p:]))
            after = tuple(sizes[i] for i in sorted(order[p + 1 :]))
            if p > 0:
                scratch[f"sum{f}_{p}"] = pltpu.VMEM(left + (r, LANES), jnp.bfloat16)
            scratch[f"got{f}_{p}"] = pltpu.VMEM((sizes[order[p]] - 1,) + after + (r, LANES), jnp.bfloat16)

    any_spec = pl.BlockSpec(memory_space=pl.ANY)
    vmem_spec = pl.BlockSpec(memory_space=pltpu.VMEM)
    part = jax.ShapeDtypeStruct((block, LANES), jnp.float32)
    names = list(scratch)

    def body(*refs):
        kernel(digits, flow_orders, r, *refs[:8], dict(zip(names, refs[8:])))

    new_master, new_first, new_second, weights = pl.pallas_call(
        body,
        name="average_update",
        out_shape=(part, part, part, jax.ShapeDtypeStruct(sizes + (block, LANES), jnp.bfloat16)),
        in_specs=[any_spec] * 4,
        out_specs=(vmem_spec,) * 4,
        scratch_shapes=[scratch[name] for name in names],
        compiler_params=pltpu.CompilerParams(
            collective_id=0, has_side_effects=True, vmem_limit_bytes=40 * 1024 * 1024
        ),
    )(grad.reshape(sizes + (block, LANES)), to_rows(master_params), to_rows(first_moment), to_rows(second_moment))
    return (
        from_rows(new_master, layers),
        from_rows(new_first, layers),
        from_rows(new_second, layers),
        from_rows(weights.reshape(devices * block, LANES), layers),
    )


def solution(mesh):
    digits = digits_of(mesh.shape["row"], mesh.shape["col"])
    in_specs = (
        P(("row", "col"), None, None),
        P(None, ("row", "col")),
        P(None, ("row", "col")),
        P(None, ("row", "col")),
    )
    out_specs = (P(None, ("row", "col")), P(None, ("row", "col")), P(None, ("row", "col")), P())
    return jax.shard_map(
        functools.partial(shards, digits), mesh=mesh, in_specs=in_specs, out_specs=out_specs, check_vma=False
    )
```

time: 171 us -> 50.1 us (0.29)
  blocking collectives: 94.1 us -> 0 us
  waiting for transfers between devices: 55.6 us -> 0 us
  Pallas kernels: 0 us -> 41.7 us
  between operations: 14.1 us -> 0.65 us
  local copies, waits for them, and re-layouts: 4.44 us -> 7.58 us
  other arithmetic: 2.1 us -> 0 us
    unnamed x1 -> x0, blocking collectives: 94.1 us -> none
    all_gather x1 -> x0, waiting for transfers between devices: 55.6 us -> none  [shards(): lax.all_gather(pieces, ('row', 'col'), axis=1, tiled=True)]
    pallas_call x0 -> x1, Pallas kernels: none -> 41.7 us  [shards(): pl.pallas_call(body, name='average_update', out_shape=(part, part, part,...]
    unnamed x7 -> x12, local copies, waits for them, and re-layouts: 4.44 us -> 7.58 us
    convert_element_type x1 -> x0, other arithmetic: 2.1 us -> none  [shards(): rounded = new_master.astype(jnp.bfloat16)]
  transfers between devices with their start and end apart: 1 -> 0, of which waited for: 1 -> 0; matrix products, arithmetic and copies ran while one was open for 0% -> 0% of each run, Pallas kernels for 0% -> 0%
where the time goes in v1:
time: 50.1 us; the launch traced here: 49.9 us
  Pallas kernels  41.7 us (83%)
  local copies, waits for them, and re-layouts  7.58 us (15%)
  between operations  0.65 us (1%)
    pallas_call x1, Pallas kernels, shards(): pl.pallas_call(body, name='average_update', out_shape=(part, part, part,...  41.7 us
    unnamed x12, local copies, waits for them, and re-layouts  7.58 us

profile of v1, /device:TPU:0, one launch (start us, length us, event | category | flops | bytes accessed | tf_op | source)
XLA Modules:
  0.0 49.9 jit_solution(12238139021110766480)
XLA Ops:
  0.6 0.0 copy-start
  0.6 1.6 %copy-done = bf16[1,2,524288]{2,1,0:T(2,128)(2,1)S(1)} copy-done((bf16[1,2,524288]{2,1,0:T(2,128)(2,1)S(1)}, bf16[1,2,524288]{2,1,0:T(2,128)(2,1)}, u32[]{:S(2)}) %copy-start) | copy-done | bytes 2097176
  2.2 0.0 copy-start.1
  2.2 0.9 %copy-done.1 = f32[2,16384]{1,0:T(2,128)S(1)} copy-done((f32[2,16384]{1,0:T(2,128)S(1)}, f32[2,16384]{1,0:T(2,128)}, u32[]{:S(2)}) %copy-start.1) | copy-done | bytes 131096
  3.1 0.0 copy-start.2
  3.1 0.9 %copy-done.2 = f32[2,16384]{1,0:T(2,128)S(1)} copy-done((f32[2,16384]{1,0:T(2,128)S(1)}, f32[2,16384]{1,0:T(2,128)}, u32[]{:S(2)}) %copy-start.2) | copy-done | bytes 131096
  4.0 0.0 copy-start.3
  4.0 0.9 %copy-done.3 = f32[2,16384]{1,0:T(2,128)S(1)} copy-done((f32[2,16384]{1,0:T(2,128)S(1)}, f32[2,16384]{1,0:T(2,128)}, u32[]{:S(2)}) %copy-start.3) | copy-done | bytes 131096
  4.9 41.7 %average_update.1 = (f32[256,128]{1,0:T(8,128)S(1)}, f32[256,128]{1,0:T(8,128)S(1)}, f32[256,128]{1,0:T(8,128)S(1)}, bf16[4,2,2,2,256,128]{5,4,3,2,1,0:T(8,128)(2,1)S(1)}) custom-call(bf16[4,2,2,2,256,128]{5,4,3,2,1,0:T(8,128)(2,1)S(1)} %bitcast.40, f32[256,128]{1,0:T(8,128)S(1)} %bitcast.42, f32[256,128]{1,0:T(8,128)S(1)} %bitcast.43, f32[256,128]{1,0:T(8,128)S(1)} %bitcast.44), custom_call_target="tpu_custom_call" | custom-call | tf_op jit(solution)/shard_map/average_update/pallas_call | solution.py:230
  46.6 0.7 %copy.20 = f32[2,16384]{1,0:T(2,128)} copy(f32[2,16384]{1,0:T(2,128)S(1)} %bitcast.47) | data formatting | bytes 262144
  47.3 0.7 %copy.21 = f32[2,16384]{1,0:T(2,128)} copy(f32[2,16384]{1,0:T(2,128)S(1)} %bitcast.46) | data formatting | bytes 262144
  47.9 0.7 %copy.22 = f32[2,16384]{1,0:T(2,128)} copy(f32[2,16384]{1,0:T(2,128)S(1)} %bitcast.45) | data formatting | bytes 262144
  48.6 1.3 %copy.23 = bf16[2,524288]{1,0:T(2,128)(2,1)} copy(bf16[2,524288]{1,0:T(2,128)(2,1)S(1)} %bitcast.41) | data formatting | bytes 4194304
Async XLA Ops:
  0.6 1.6 %copy-start = (bf16[1,2,524288]{2,1,0:T(2,128)(2,1)S(1)}, bf16[1,2,524288]{2,1,0:T(2,128)(2,1)}, u32[]{:S(2)}) copy-start(bf16[1,2,524288]{2,1,0:T(2,128)(2,1)} %param.4) | copy-start | bytes 6291460
  2.2 0.9 %copy-start.1 = (f32[2,16384]{1,0:T(2,128)S(1)}, f32[2,16384]{1,0:T(2,128)}, u32[]{:S(2)}) copy-start(f32[2,16384]{1,0:T(2,128)} %param.5) | copy-start | bytes 393220
  3.1 0.9 %copy-start.2 = (f32[2,16384]{1,0:T(2,128)S(1)}, f32[2,16384]{1,0:T(2,128)}, u32[]{:S(2)}) copy-start(f32[2,16384]{1,0:T(2,128)} %param.6) | copy-start | bytes 393220
  4.0 0.9 %copy-start.3 = (f32[2,16384]{1,0:T(2,128)S(1)}, f32[2,16384]{1,0:T(2,128)}, u32[]{:S(2)}) copy-start(f32[2,16384]{1,0:T(2,128)} %param.7) | copy-start | bytes 393220

commit v2 on v1

--- a/solution.py
+++ b/solution.py
@@ -17,6 +17,7 @@
 
 LANES = 128
 FLOWS = 4
+VMEM_LIMIT = 40 * 1024 * 1024
 MESH = pl.DeviceIdType.MESH
 
 
@@ -76,16 +77,20 @@
     flows = len(flow_orders)
     rows = [pl.ds(f * r, r) for f in range(flows)]
 
-    loads = []
-    for f in range(flows):
-        digit = flow_orders[f][0]
-        where = tuple(mine[i] if i == digit else slice(None) for i in range(count)) + (rows[f],)
-        copy = pltpu.make_async_copy(grad.at[where], scratch["own"].at[f], scratch["load_sem"].at[f])
-        copy.start()
-        loads.append(copy)
+    loads = {}
+    for keep in (0, 1):
+        for f in range(flows):
+            digit = flow_orders[f][0]
+            for t in [0] if keep else range(1, digits[digit][1]):
+                value = peer(digit, t)[0]
+                where = tuple(value if i == digit else slice(None) for i in range(count)) + (rows[f],)
+                loads[f, t] = pltpu.make_async_copy(
+                    grad.at[where], scratch[f"raw{f}"].at[t], scratch["load_sem"].at[f, t]
+                )
+                loads[f, t].start()
     states = []
     for i, (src, name) in enumerate(((master, "master"), (first, "first"), (second, "second"))):
-        copy = pltpu.make_async_copy(src, scratch[name], scratch["load_sem"].at[flows + i])
+        copy = pltpu.make_async_copy(src, scratch[name], scratch["state_sem"].at[i])
         copy.start()
         states.append(copy)
 
@@ -113,13 +118,29 @@
         sent.append(copy)
         pending.setdefault((f, step), []).append(copy)
 
+    def total(f, p, place):
+        order = flow_orders[f]
+        value = scratch[f"raw{f}"][(0,) + tuple(place.get(i, mine[i]) for i in sorted(order[1:]))].astype(jnp.float32)
+        for q in range(p):
+            after = tuple(place.get(i, mine[i]) for i in sorted(order[q + 1 :]))
+            for t in range(digits[order[q]][1] - 1):
+                value += scratch[f"got{f}_{q}"][(t,) + after].astype(jnp.float32)
+        return value
+
     def scatter(f, p):
         digit = flow_orders[f][p]
-        left = sorted(flow_orders[f][p:])
+        after = sorted(flow_orders[f][p + 1 :])
         for t in range(1, digits[digit][1]):
             value, device = peer(digit, t)
-            where = tuple(value if i == digit else slice(None) for i in left)
-            src = grad.at[where + (rows[f],)] if p == 0 else scratch[f"sum{f}_{p}"].at[where]
+            if p == 0:
+                loads[f, t].wait()
+                src = scratch[f"raw{f}"].at[t]
+            else:
+                src = scratch[f"sum{f}_{p}"].at[t - 1]
+                for idx in np.ndindex(*(digits[i][1] for i in after)):
+                    place = dict(zip(after, idx))
+                    place[digit] = value
+                    src[idx] = total(f, p, place).astype(jnp.bfloat16)
             send(f, p, digit, t, src, scratch[f"got{f}_{p}"].at[t - 1], device)
 
     def gather(f, p):
@@ -137,34 +158,20 @@
         scatter(f, 0)
     for p in range(count):
         for f in range(flows):
-            digit = flow_orders[f][p]
-            left = sorted(flow_orders[f][p:])
-            after = sorted(flow_orders[f][p + 1 :])
             if p == 0:
-                loads[f].wait()
+                loads[f, 0].wait()
             arrived(f, p)
-            got = scratch[f"got{f}_{p}"]
-            last = p == count - 1
-            for idx in np.ndindex(*(digits[i][1] for i in after)):
-                if p == 0:
-                    total = scratch["own"][(f,) + idx].astype(jnp.float32)
-                else:
-                    place = dict(zip(after, idx))
-                    total = scratch[f"sum{f}_{p}"][
-                        tuple(mine[digit] if i == digit else place[i] for i in left)
-                    ].astype(jnp.float32)
-                for t in range(digits[digit][1] - 1):
-                    total += got[(t,) + idx].astype(jnp.float32)
-                if not last:
-                    scratch[f"sum{f}_{p + 1}"][idx] = total.astype(jnp.bfloat16)
-            if not last:
+            if p < count - 1:
                 scatter(f, p + 1)
                 continue
             if f == 0:
                 for copy in states:
                     copy.wait()
             updated, moment, variance = adam_update(
-                total / devices, scratch["master"][rows[f], :], scratch["first"][rows[f], :], scratch["second"][rows[f], :]
+                total(f, count, {}) / devices,
+                scratch["master"][rows[f], :],
+                scratch["first"][rows[f], :],
+                scratch["second"][rows[f], :],
             )
             weights[tuple(mine) + (rows[f],)] = updated.astype(jnp.bfloat16)
             gather(f, count - 1)
@@ -190,6 +197,27 @@
     return x.reshape(total // layers, layers, LANES).transpose(1, 0, 2).reshape(layers, total // layers * LANES)
 
 
+def write_out(*arrays):
+    count = len(arrays)
+
+    def body(*refs):
+        copies = [pltpu.make_async_copy(refs[i], refs[count + i], refs[-1].at[i]) for i in range(count)]
+        for copy in copies[::-1]:
+            copy.start()
+        for copy in copies:
+            copy.wait()
+
+    return pl.pallas_call(
+        body,
+        name="write_out",
+        out_shape=tuple(jax.ShapeDtypeStruct(x.shape, x.dtype) for x in arrays),
+        in_specs=[pl.BlockSpec(memory_space=pltpu.VMEM)] * count,
+        out_specs=(pl.BlockSpec(memory_space=pltpu.HBM),) * count,
+        scratch_shapes=[pltpu.SemaphoreType.DMA((count,))],
+        compiler_params=pltpu.CompilerParams(vmem_limit_bytes=1 << 20),
+    )(*arrays)
+
+
 def shards(digits, gradients, master_params, first_moment, second_moment):
     count = len(digits)
     sizes = tuple(d[1] for d in digits)
@@ -204,8 +232,8 @@
 
     most = max(sizes) - 1
     scratch = {
-        "own": pltpu.VMEM((flows,) + sizes[:-1] + (r, LANES), jnp.bfloat16),
-        "load_sem": pltpu.SemaphoreType.DMA((flows + 3,)),
+        "load_sem": pltpu.SemaphoreType.DMA((flows, most + 1)),
+        "state_sem": pltpu.SemaphoreType.DMA((3,)),
         "send_sem": pltpu.SemaphoreType.DMA((flows, 2 * count, most)),
         "recv_sem": pltpu.SemaphoreType.DMA((flows, 2 * count, most)),
     }
@@ -213,13 +241,14 @@
         scratch[name] = pltpu.VMEM((block, LANES), jnp.float32)
     for f, order in enumerate(flow_orders):
         for p in range(count):
-            left = tuple(sizes[i] for i in sorted(order[p:]))
-            after = tuple(sizes[i] for i in sorted(order[p + 1 :]))
-            if p > 0:
-                scratch[f"sum{f}_{p}"] = pltpu.VMEM(left + (r, LANES), jnp.bfloat16)
-            scratch[f"got{f}_{p}"] = pltpu.VMEM((sizes[order[p]] - 1,) + after + (r, LANES), jnp.bfloat16)
-
-    any_spec = pl.BlockSpec(memory_space=pl.ANY)
+            after = tuple(sizes[i] for i in sorted(order[p + 1 :])) + (r, LANES)
+            if p == 0:
+                scratch[f"raw{f}"] = pltpu.VMEM((sizes[order[p]],) + after, jnp.bfloat16)
+            else:
+                scratch[f"sum{f}_{p}"] = pltpu.VMEM((sizes[order[p]] - 1,) + after, jnp.bfloat16)
+            scratch[f"got{f}_{p}"] = pltpu.VMEM((sizes[order[p]] - 1,) + after, jnp.bfloat16)
+
+    hbm_spec = pl.BlockSpec(memory_space=pltpu.HBM)
     vmem_spec = pl.BlockSpec(memory_space=pltpu.VMEM)
     part = jax.ShapeDtypeStruct((block, LANES), jnp.float32)
     names = list(scratch)
@@ -231,19 +260,25 @@
         body,
         name="average_update",
         out_shape=(part, part, part, jax.ShapeDtypeStruct(sizes + (block, LANES), jnp.bfloat16)),
-        in_specs=[any_spec] * 4,
+        in_specs=[hbm_spec] * 4,
         out_specs=(vmem_spec,) * 4,
         scratch_shapes=[scratch[name] for name in names],
         compiler_params=pltpu.CompilerParams(
-            collective_id=0, has_side_effects=True, vmem_limit_bytes=40 * 1024 * 1024
+            collective_id=0, has_side_effects=True, vmem_limit_bytes=VMEM_LIMIT
         ),
-    )(grad.reshape(sizes + (block, LANES)), to_rows(master_params), to_rows(first_moment), to_rows(second_moment))
-    return (
-        from_rows(new_master, layers),
-        from_rows(new_first, layers),
-        from_rows(new_second, layers),
-        from_rows(weights.reshape(devices * block, LANES), layers),
-    )
+    )(
+        *(
+            pltpu.with_memory_space_constraint(x, pltpu.HBM)
+            for x in (
+                grad.reshape(sizes + (block, LANES)),
+                to_rows(master_params),
+                to_rows(first_moment),
+                to_rows(second_moment),
+            )
+        )
+    )
+    results = write_out(new_master, new_first, new_second, weights.reshape(devices * block, LANES))
+    return tuple(from_rows(x, layers) for x in results)
 
 
 def solution(mesh):

time: 50.1 us -> 43.1 us (0.86)
  local copies, waits for them, and re-layouts: 7.58 us -> 0 us
  Pallas kernels: 41.7 us -> 42.3 us
    unnamed x12 -> x0, local copies, waits for them, and re-layouts: 7.58 us -> none
    pallas_call x0 -> x1, Pallas kernels: none -> 1.47 us  [write_out(): pl.pallas_call(body, name='write_out', out_shape=tuple((jax.ShapeDtypeStr...]
    pallas_call x1, Pallas kernels: 41.7 us -> 40.9 us  [shards(): pl.pallas_call(body, name='average_update', out_shape=(part, part, part,...]
where the time goes in v2:
time: 43.1 us; the launch traced here: 43 us
  Pallas kernels  42.3 us (98%)
  between operations  0.64 us (1%)
    pallas_call x1, Pallas kernels, shards(): pl.pallas_call(body, name='average_update', out_shape=(part, part, part,...  40.9 us
    pallas_call x1, Pallas kernels, write_out(): pl.pallas_call(body, name='write_out', out_shape=tuple((jax.ShapeDtypeStr...  1.47 us

profile of v2, /device:TPU:0, one launch (start us, length us, event | category | flops | bytes accessed | tf_op | source)
XLA Modules:
  0.0 43.0 jit_solution(15257686078816447524)
XLA Ops:
  0.6 40.9 %average_update.1 = (f32[256,128]{1,0:T(8,128)S(1)}, f32[256,128]{1,0:T(8,128)S(1)}, f32[256,128]{1,0:T(8,128)S(1)}, bf16[4,2,2,2,256,128]{5,4,3,2,1,0:T(8,128)(2,1)S(1)}) custom-call(bf16[4,2,2,2,256,128]{5,4,3,2,1,0:T(8,128)(2,1)} %bitcast.42, f32[256,128]{1,0:T(8,128)} %bitcast.43, f32[256,128]{1,0:T(8,128)} %bitcast.44, f32[256,128]{1,0:T(8,128)} %bitcast.45), custom_call_target="tpu_custom_call" | custom-call | tf_op jit(solution)/shard_map/average_update/pallas_call | solution.py:259
  41.5 1.5 %write_out.1 = (f32[256,128]{1,0:T(8,128)}, f32[256,128]{1,0:T(8,128)}, f32[256,128]{1,0:T(8,128)}, bf16[8192,128]{1,0:T(8,128)(2,1)}) custom-call(f32[256,128]{1,0:T(8,128)S(1)} %get-tuple-element.12.refs_0_, f32[256,128]{1,0:T(8,128)S(1)} %get-tuple-element.13.refs_1_, f32[256,128]{1,0:T(8,128)S(1)} %get-tuple-element.14.refs_2_, ...), custom_call_target="tpu_custom_call" | custom-call | tf_op jit(solution)/shard_map/write_out/pallas_call | solution.py:210

commit v3 on v2

--- a/solution.py
+++ b/solution.py
@@ -16,7 +16,8 @@
 adam_step = 10.0
 
 LANES = 128
-FLOWS = 4
+SPLIT = ((56, "x"), (56, "y"), (48, "x"), (48, "y"), (48, "z"))
+STEP_ROWS = 8
 VMEM_LIMIT = 40 * 1024 * 1024
 MESH = pl.DeviceIdType.MESH
 
@@ -58,10 +59,10 @@
     col_at = [i for i in range(last) if digits[i][0] == "col"]
     x, y = row_at[-1:], col_at[:1]
     rest = col_at[1:] + row_at[:-1]
-    return ([last] + x + y + rest, [last] + y + x + rest)
-
-
-def kernel(digits, flow_orders, r, grad, master, first, second, new_master, new_first, new_second, weights, scratch):
+    return {"x": [last] + x + y + rest, "y": [last] + y + x + rest, "z": [last] + rest + x + y, "w": [last] + rest + y + x}
+
+
+def kernel(digits, flow_orders, rows, grad, master, first, second, new_master, new_first, new_second, weights, scratch):
     count = len(digits)
     devices = int(np.prod([d[1] for d in digits]))
     at = {axis: lax.axis_index(axis) for axis in ("row", "col")}
@@ -75,7 +76,6 @@
         return value, (ids["row"], ids["col"])
 
     flows = len(flow_orders)
-    rows = [pl.ds(f * r, r) for f in range(flows)]
 
     loads = {}
     for keep in (0, 1):
@@ -156,33 +156,33 @@
 
     for f in range(flows):
         scatter(f, 0)
-    for p in range(count):
-        for f in range(flows):
-            if p == 0:
-                loads[f, 0].wait()
-            arrived(f, p)
-            if p < count - 1:
-                scatter(f, p + 1)
-                continue
-            if f == 0:
-                for copy in states:
-                    copy.wait()
-            updated, moment, variance = adam_update(
-                total(f, count, {}) / devices,
-                scratch["master"][rows[f], :],
-                scratch["first"][rows[f], :],
-                scratch["second"][rows[f], :],
-            )
-            weights[tuple(mine) + (rows[f],)] = updated.astype(jnp.bfloat16)
-            gather(f, count - 1)
-            new_master[rows[f], :] = updated
-            new_first[rows[f], :] = moment
-            new_second[rows[f], :] = variance
-    for p in reversed(range(count)):
-        for f in range(flows):
-            arrived(f, 2 * count - 1 - p)
-            if p > 0:
-                gather(f, p - 1)
+    def update(f):
+        if f == 0:
+            for copy in states:
+                copy.wait()
+        updated, moment, variance = adam_update(
+            total(f, count, {}) / devices,
+            scratch["master"][rows[f], :],
+            scratch["first"][rows[f], :],
+            scratch["second"][rows[f], :],
+        )
+        weights[tuple(mine) + (rows[f],)] = updated.astype(jnp.bfloat16)
+        gather(f, count - 1)
+        new_master[rows[f], :] = updated
+        new_first[rows[f], :] = moment
+        new_second[rows[f], :] = variance
+
+    turns = [(step, f) for step in range(2 * count) for f in range(flows)]
+    for step, f in turns:
+        if step == 0:
+            loads[f, 0].wait()
+        arrived(f, step)
+        if step < count - 1:
+            scatter(f, step + 1)
+        elif step == count - 1:
+            update(f)
+        elif step < 2 * count - 1:
+            gather(f, 2 * count - 2 - step)
     for copy in sent:
         copy.wait_send()
 
@@ -225,10 +225,17 @@
     layers = gradients.shape[1]
     grad = to_rows(gradients[0])
     block = grad.shape[0] // devices
-    flows = next(n for n in (FLOWS, 2, 1) if block % n == 0 and (block // n) % 16 == 0)
-    r = block // flows
     orders = orders_of(digits)
-    flow_orders = [orders[f % len(orders)] for f in range(flows)]
+    whole, start, done = sum(share for share, _ in SPLIT), 0, 0
+    flow_orders, rows = [], []
+    for share, name in SPLIT:
+        done += share
+        end = block if done == whole else done * block // whole // STEP_ROWS * STEP_ROWS
+        if end > start:
+            flow_orders.append(orders[name])
+            rows.append(pl.ds(start, end - start))
+            start = end
+    flows = len(rows)
 
     most = max(sizes) - 1
     scratch = {
@@ -241,7 +248,7 @@
         scratch[name] = pltpu.VMEM((block, LANES), jnp.float32)
     for f, order in enumerate(flow_orders):
         for p in range(count):
-            after = tuple(sizes[i] for i in sorted(order[p + 1 :])) + (r, LANES)
+            after = tuple(sizes[i] for i in sorted(order[p + 1 :])) + (rows[f].size, LANES)
             if p == 0:
                 scratch[f"raw{f}"] = pltpu.VMEM((sizes[order[p]],) + after, jnp.bfloat16)
             else:
@@ -254,7 +261,7 @@
     names = list(scratch)
 
     def body(*refs):
-        kernel(digits, flow_orders, r, *refs[:8], dict(zip(names, refs[8:])))
+        kernel(digits, flow_orders, rows, *refs[:8], dict(zip(names, refs[8:])))
 
     new_master, new_first, new_second, weights = pl.pallas_call(
         body,

time: 43.1 us -> 40.1 us (0.930)
  Pallas kernels: 42.3 us -> 39.3 us
    pallas_call x1, Pallas kernels: 40.9 us -> 37.9 us  [shards(): pl.pallas_call(body, name='average_update', out_shape=(part, part, part,...]
where the time goes in v3:
time: 40.1 us; the launch traced here: 40 us
  Pallas kernels  39.3 us (98%)
  between operations  0.64 us (2%)
    pallas_call x1, Pallas kernels, shards(): pl.pallas_call(body, name='average_update', out_shape=(part, part, part,...  37.9 us
    pallas_call x1, Pallas kernels, write_out(): pl.pallas_call(body, name='write_out', out_shape=tuple((jax.ShapeDtypeStr...  1.47 us

profile of v3, /device:TPU:0, one launch (start us, length us, event | category | flops | bytes accessed | tf_op | source)
XLA Modules:
  0.0 40.0 jit_solution(9543809625517997762)
XLA Ops:
  0.6 37.9 %average_update.1 = (f32[256,128]{1,0:T(8,128)S(1)}, f32[256,128]{1,0:T(8,128)S(1)}, f32[256,128]{1,0:T(8,128)S(1)}, bf16[4,2,2,2,256,128]{5,4,3,2,1,0:T(8,128)(2,1)S(1)}) custom-call(bf16[4,2,2,2,256,128]{5,4,3,2,1,0:T(8,128)(2,1)} %bitcast.42, f32[256,128]{1,0:T(8,128)} %bitcast.43, f32[256,128]{1,0:T(8,128)} %bitcast.44, f32[256,128]{1,0:T(8,128)} %bitcast.45), custom_call_target="tpu_custom_call" | custom-call | tf_op jit(solution)/shard_map/average_update/pallas_call | solution.py:266
  38.5 1.5 %write_out.1 = (f32[256,128]{1,0:T(8,128)}, f32[256,128]{1,0:T(8,128)}, f32[256,128]{1,0:T(8,128)}, bf16[8192,128]{1,0:T(8,128)(2,1)}) custom-call(f32[256,128]{1,0:T(8,128)S(1)} %get-tuple-element.12.refs_0_, f32[256,128]{1,0:T(8,128)S(1)} %get-tuple-element.13.refs_1_, f32[256,128]{1,0:T(8,128)S(1)} %get-tuple-element.14.refs_2_, ...), custom_call_target="tpu_custom_call" | custom-call | tf_op jit(solution)/shard_map/write_out/pallas_call | solution.py:210
